TPU v7x, 32 devices: a whole 2x2x4 slice. The times are simulated.
32 devices in a mesh: floor: 4 (over y, x), zone: 8 (over z, core).
Axes of the slice: x: 2, y: 2, z: 4, core: 2. Of those that a mesh axis runs over, the one named last changes fastest.
Arguments:
- factor: float32 [512, 96, 384], P(('floor', 'zone')), may hold values from -0.625 to 0.625
- plant_map: float32 [512, 96, 384], P(('floor', 'zone')), may hold values from -0.4082483 to 0.4082483
- offset: float32 [512, 384], P(('floor', 'zone')), may hold values from -10 to 10
- start_plan: float32 [512, 384], P(('floor', 'zone')), may hold values from -10 to 10
- demand: float32 [4, 48], replicated, may hold values from -768 to 768
- start_price: float32 [4, 48], replicated, may hold values from -6 to 6
- start_multiplier: float32 [512, 48], P(('floor', 'zone')), may hold values from -6 to 6
- neighbors: int32 [512, 4], P(('floor', 'zone')), may hold values from 0 to 127
- loop_of_zone: int32 [512], P(('floor', 'zone')), may hold values from 0 to 3
Outputs:
- control: float32 [512, 384], P(('floor', 'zone'))
- price: float32 [4, 48], replicated
- multiplier: float32 [512, 48], P(('floor', 'zone'))
Inputs may be any that keep to these rules, and one draw needn't show every extreme that they name: `neighbors`: indices count zones within the zone's own floor of 128 consecutive zones.
All inputs are finite; a program needn't handle non-finite values.
Results may differ from a plain program's by a relative error of at most 0.0001.
Values sent between devices are 32-bit elements; how exact they have to be, the bound alone decides.
No kernel may reach another device: no remote copies, remote signals or barrier semaphores. Data moves between devices by JAX's collectives and lax.ppermute only.
A program may use at most 64 MiB of HBM per device.

v0:
```python
import jax
import jax.numpy as jnp
from jax import lax
from jax.sharding import PartitionSpec as P

HORIZON = 48
NEIGHBORS = 4
LOOPS = 4
ITERS = 2


def select_rows(neighbors, count):
    columns = jnp.arange(count, dtype=jnp.int32)
    picks = (neighbors[:, :, None] == columns[None, None, :]).astype(jnp.float32)
    return jnp.sum(picks, axis=1) / NEIGHBORS


def local(
    factor,
    plant_map,
    offset,
    start_plan,
    demand,
    start_price,
    start_multiplier,
    neighbors,
    loop_of_zone,
):
    control = start_plan
    price = start_price
    multiplier = start_multiplier
    zones_here = control.shape[0]
    zones_all = zones_here * lax.axis_size("floor") * lax.axis_size("zone")
    onehot = (loop_of_zone[:, None] == jnp.arange(LOOPS, dtype=jnp.int32)[None, :]).astype(
        jnp.float32
    )
    for step in range(ITERS):
        outputs = jnp.einsum("zkv,zv->zk", plant_map, control, precision=lax.Precision.HIGHEST)
        shares = outputs[:, :HORIZON]
        bound = outputs[:, HORIZON:]
        partial_load = jnp.dot(onehot.T, shares, precision=lax.Precision.HIGHEST)
        floor_load = lax.psum(partial_load, "zone")
        total = lax.psum(floor_load, "floor")
        excess = (total - demand) * (LOOPS / zones_all)
        shift = jnp.dot(onehot, excess + price, precision=lax.Precision.HIGHEST)
        price = price + excess
        target_share = shares - shift
        floor_bound = lax.all_gather(bound, "zone", axis=0, tiled=True)
        weights = select_rows(neighbors, floor_bound.shape[0])
        near = jnp.dot(weights, floor_bound, precision=lax.Precision.HIGHEST)
        target_bound = (bound + near) / 2.0 - multiplier
        multiplier = multiplier + (bound - near) / 2.0
        target = jnp.concatenate([target_share, target_bound], axis=1)
        control = (
            0.8 * jnp.einsum("zkv,zk->zv", factor, target, precision=lax.Precision.HIGHEST) - offset
        )
    return (control, price, multiplier)


def solution(mesh):
    placed = (
        P(("floor", "zone"), None, None),
        P(("floor", "zone"), None, None),
        P(("floor", "zone"), None),
        P(("floor", "zone"), None),
        P(),
        P(),
        P(("floor", "zone"), None),
        P(("floor", "zone"), None),
        P(("floor", "zone")),
    )
    return jax.shard_map(
        local,
        mesh=mesh,
        in_specs=placed,
        out_specs=(P(("floor", "zone"), None), P(), P(("floor", "zone"), None)),
        check_vma=False,
    )
```

profile of v0, /device:TPU:0, one launch (start us, length us, event | category | flops | bytes accessed | tf_op | source)
XLA Modules:
  0.0 91.8 jit_solution(17976281189199001725)
XLA Ops:
  0.6 0.0 copy-start
  0.6 0.0 copy-start.3
  0.7 0.0 copy-start.4
  0.7 0.0 copy-start.8
  0.7 0.0 copy-start.5
  0.7 0.0 copy-start.6
  0.7 0.0 copy-start.2
  0.7 4.4 %fusion.5 = f32[16,1,96]{2,1,0:T(1,128)S(1)} fusion(f32[16,96,384]{2,1,0:T(8,128)} %param.10, f32[16,384,1]{1,0,2:T(8,128)} %bitcast.43), kind=kOutput, calls=%fused_computation.11 | convolution fusion | flops 7077888 | bytes 2390016 | tf_op jit(solution)/shard_map/zkv,zv->zk/dot_general | solution.py:38
  5.1 0.1 slice.17
  5.2 15.7 %all_gather.6 = f32[128,48]{1,0:T(8,128)S(1)} all-gather(f32[16,48]{1,0:T(8,128)S(1)} %slice.17), channel_id=1, replica_groups=mesh['floor'=4,'zone'=8] {'zone'}, dimensions={0}, use_global_device_ids=true | all-gather | bytes 27648 | tf_op jit(solution)/shard_map/all_gather | solution.py:48
  20.9 0.0 copy-done.4
  20.9 0.1 convert_reduce_fusion
  21.0 0.0 copy-done.3
  21.0 0.2 multiply_subtract_fusion.1
  21.1 0.0 copy-done.8
  21.1 0.3 fusion.8
  21.4 16.9 %psum.28 = f32[4,48]{1,0:T(4,128)S(1)} all-reduce(f32[4,48]{1,0:T(4,128)S(1)} %fusion.8), channel_id=1, replica_groups=mesh['floor'=4,'zone'=8] {'zone'}, use_global_device_ids=true, to_apply=%region_0.0 | all-reduce | flops 192 | bytes 1536 | tf_op jit(solution)/shard_map/psum | solution.py:42
  38.3 9.9 %psum.29 = f32[4,48]{1,0:T(4,128)S(1)} all-reduce(f32[4,48]{1,0:T(4,128)S(1)} %psum.28), channel_id=1, replica_groups=mesh['floor'=4,'zone'=8] {'floor'}, use_global_device_ids=true, to_apply=%region_1.0 | all-reduce | flops 192 | bytes 1536 | tf_op jit(solution)/shard_map/psum | solution.py:43
  48.2 0.0 copy-done.5
  48.2 0.0 copy-done.6
  48.2 0.0 copy-start.1
  48.2 0.2 convolution_subtract_fusion.1
  48.4 0.1 pad_maximum_fusion
  48.5 0.0 copy-done
  48.5 1.4 %fusion.24 = f32[16,1,384]{2,1,0:T(1,128)S(1)} fusion(f32[16,96,1]{1,2,0:T(1,128)S(1)} %bitcast.41, f32[16,96,384]{2,1,0:T(8,128)S(1)} %copy-done), kind=kOutput, calls=%fused_computation.39 | convolution fusion | flops 7077888 | bytes 2390016 | tf_op jit(solution)/shard_map/zkv,zk->zv/dot_general | solution.py:55
  49.9 0.0 copy-done.2
  49.9 0.0 copy-done.1
  49.9 2.6 %fusion.3 = f32[16,1,96]{2,1,0:T(1,128)S(1)} fusion(f32[16,96,384]{2,1,0:T(8,128)S(1)} %copy-done.1, f32[16,384,1]{1,0,2:T(8,128)S(1)} %fusion.2), kind=kOutput, calls=%fused_computation.9 | convolution fusion | flops 7077888 | bytes 2390016 | tf_op jit(solution)/shard_map/zkv,zv->zk/dot_general | solution.py:38
  52.5 0.1 slice.19
  52.6 14.0 %all_gather.7 = f32[128,48]{1,0:T(8,128)S(1)} all-gather(f32[16,48]{1,0:T(8,128)S(1)} %slice.19), channel_id=1, replica_groups=mesh['floor'=4,'zone'=8] {'zone'}, dimensions={0}, use_global_device_ids=true | all-gather | bytes 27648 | tf_op jit(solution)/shard_map/all_gather | solution.py:48
  66.6 0.8 multiply_add_fusion
  67.4 0.3 fusion.7
  67.6 13.9 %psum.30 = f32[4,48]{1,0:T(4,128)S(1)} all-reduce(f32[4,48]{1,0:T(4,128)S(1)} %fusion.7), channel_id=1, replica_groups=mesh['floor'=4,'zone'=8] {'zone'}, use_global_device_ids=true, to_apply=%region_3.0 | all-reduce | flops 192 | bytes 1536 | tf_op jit(solution)/shard_map/psum | solution.py:42
  81.5 7.9 %psum.31 = f32[4,48]{1,0:T(4,128)S(1)} all-reduce(f32[4,48]{1,0:T(4,128)S(1)} %psum.30), channel_id=1, replica_groups=mesh['floor'=4,'zone'=8] {'floor'}, use_global_device_ids=true, to_apply=%region_4.0 | all-reduce | flops 192 | bytes 1536 | tf_op jit(solution)/shard_map/psum | solution.py:43
  89.5 0.0 copy-start.7
  89.5 0.2 convolution_subtract_fusion
  89.7 0.1 pad_maximum_fusion.1
  89.8 1.4 %fusion.25 = f32[16,1,384]{2,1,0:T(1,128)S(1)} fusion(f32[16,96,1]{1,2,0:T(1,128)S(1)} %bitcast.42, f32[16,96,384]{2,1,0:T(8,128)S(1)} %copy-done), kind=kOutput, calls=%fused_computation.40 | convolution fusion | flops 7077888 | bytes 2390016 | tf_op jit(solution)/shard_map/zkv,zk->zv/dot_general | solution.py:55
  91.2 0.6 fusion
  91.8 0.0 copy-done.7
  (2 shorter events, 0.0 us)
Async XLA Ops:
  0.6 47.8 %copy-start = (f32[16,96,384]{2,1,0:T(8,128)S(1)}, f32[16,96,384]{2,1,0:T(8,128)}, u32[]{:S(2)}) copy-start(f32[16,96,384]{2,1,0:T(8,128)} %param.9) | copy-start | bytes 7077892
  0.6 20.3 %copy-start.3 = (f32[16,48]{1,0:T(8,128)S(1)}, f32[16,48]{1,0:T(8,128)}, u32[]{:S(2)}) copy-start(f32[16,48]{1,0:T(8,128)} %param.15) | copy-start | bytes 9220
  0.7 20.2 %copy-start.4 = (s32[16,4]{0,1:T(4,128)S(1)}, s32[16,4]{0,1:T(4,128)}, u32[]{:S(2)}) copy-start(s32[16,4]{0,1:T(4,128)} %param.16) | copy-start | bytes 772
  0.7 20.5 %copy-start.8 = (s32[16]{0:T(128)S(1)}, s32[16]{0:T(128)}, u32[]{:S(2)}) copy-start(s32[16]{0:T(128)} %param.17) | copy-start | bytes 196
  0.7 47.5 %copy-start.5 = (f32[4,48]{1,0:T(4,128)S(1)}, f32[4,48]{1,0:T(4,128)}, u32[]{:S(2)}) copy-start(f32[4,48]{1,0:T(4,128)} %param.14) | copy-start | bytes 2308
  0.7 47.5 %copy-start.6 = (f32[4,48]{1,0:T(4,128)S(1)}, f32[4,48]{1,0:T(4,128)}, u32[]{:S(2)}) copy-start(f32[4,48]{1,0:T(4,128)} %param.13) | copy-start | bytes 2308
  0.7 49.2 %copy-start.2 = (f32[16,384]{1,0:T(8,128)S(1)}, f32[16,384]{1,0:T(8,128)}, u32[]{:S(2)}) copy-start(f32[16,384]{1,0:T(8,128)} %param.11) | copy-start | bytes 73732
  48.2 1.7 %copy-start.1 = (f32[16,96,384]{2,1,0:T(8,128)S(1)}, f32[16,96,384]{2,1,0:T(8,128)}, u32[]{:S(2)}) copy-start(f32[16,96,384]{2,1,0:T(8,128)} %param.10) | copy-start | bytes 7077892
  89.5 2.3 %copy-start.7 = (f32[4,48]{1,0:T(4,128)}, f32[4,48]{1,0:T(4,128)S(1)}, u32[]{:S(2)}) copy-start(f32[4,48]{1,0:T(4,128)S(1)} %multiply_add_fusion.2) | copy-start | bytes 2308
where the time goes:
time: 92.1 us; the launch traced here: 91.8 us
  blocking collectives  78.3 us (85%)
  matrix products  11.7 us (13%)
    psum x2, blocking collectives, local(): floor_load = lax.psum(partial_load, 'zone')  30.8 us
    all_gather x2, blocking collectives, local(): floor_bound = lax.all_gather(bound, 'zone', axis=0, tiled=True)  29.7 us
    psum x2, blocking collectives, local(): total = lax.psum(floor_load, 'floor')  17.8 us
    dot_general x2, matrix products, local(): jnp.einsum('zkv,zv->zk', plant_map, control, precision=lax.Precision.HIGH...  7 us
    dot_general x2, matrix products, local(): jnp.einsum('zkv,zk->zv', factor, target, precision=lax.Precision.HIGHEST)  2.88 us

commit v1 on v0

--- a/solution.py
+++ b/solution.py
@@ -7,6 +7,14 @@
 NEIGHBORS = 4
 LOOPS = 4
 ITERS = 2
+
+
+def sum_by_hops(shard, axis):
+    size, total = (lax.axis_size(axis), shard)
+    for stride in [1 << k for k in range(size.bit_length() - 1)]:
+        swap = [(i, i ^ stride) for i in range(size)]
+        total = total + lax.ppermute(total, axis, swap)
+    return total
 
 
 def select_rows(neighbors, count):
@@ -40,7 +48,7 @@
         bound = outputs[:, HORIZON:]
         partial_load = jnp.dot(onehot.T, shares, precision=lax.Precision.HIGHEST)
         floor_load = lax.psum(partial_load, "zone")
-        total = lax.psum(floor_load, "floor")
+        total = sum_by_hops(floor_load, "floor")
         excess = (total - demand) * (LOOPS / zones_all)
         shift = jnp.dot(onehot, excess + price, precision=lax.Precision.HIGHEST)
         price = price + excess

time: 92.1 us -> 81.7 us (0.89)
  blocking collectives: 78.3 us -> 59.6 us
  starting transfers between devices: 0 us -> 5.17 us
  waiting for transfers between devices: 0 us -> 3.2 us
    psum x2 -> x0, blocking collectives: 17.8 us -> none  [local(): total = lax.psum(floor_load, 'floor')]
    ppermute x0 -> x4, starting transfers between devices: none -> 5.17 us  [sum_by_hops(): total = total + lax.ppermute(total, axis, swap)]
    ppermute x0 -> x4, waiting for transfers between devices: none -> 3.2 us  [sum_by_hops(): total = total + lax.ppermute(total, axis, swap)]
    all_gather x2, blocking collectives: 29.7 us -> 28 us  [local(): floor_bound = lax.all_gather(bound, 'zone', axis=0, tiled=True)]
  transfers between devices with their start and end apart: 0 -> 4, of which waited for: 0 -> 2; matrix products, arithmetic and copies ran while one was open for 0% -> 1% of each run, Pallas kernels for 0% -> 0%
where the time goes in v1:
time: 81.7 us; the launch traced here: 81.5 us
  blocking collectives  59.6 us (73%)
  matrix products  11.7 us (14%)
  starting transfers between devices  5.17 us (6%)
  waiting for transfers between devices  3.2 us (4%)
  other arithmetic  0.88 us (1%)
    psum x2, blocking collectives, local(): floor_load = lax.psum(partial_load, 'zone')  31.7 us
    all_gather x2, blocking collectives, local(): floor_bound = lax.all_gather(bound, 'zone', axis=0, tiled=True)  28 us
    dot_general x2, matrix products, local(): jnp.einsum('zkv,zv->zk', plant_map, control, precision=lax.Precision.HIGH...  7 us
    ppermute x4, starting transfers between devices, sum_by_hops(): total = total + lax.ppermute(total, axis, swap)  5.17 us
    ppermute x4, waiting for transfers between devices, sum_by_hops(): total = total + lax.ppermute(total, axis, swap)  3.2 us
    dot_general x2, matrix products, local(): jnp.einsum('zkv,zk->zv', factor, target, precision=lax.Precision.HIGHEST)  2.88 us
  transfers between devices with their start and end apart: 4, of which 2 were waited for; matrix products, arithmetic and copies ran while one was open for 1% of the time, Pallas kernels for 0%

profile of v1, /device:TPU:0, one launch (start us, length us, event | category | flops | bytes accessed | tf_op | source)
XLA Modules:
  0.0 81.5 jit_solution(13417583378962574427)
XLA Ops:
  0.6 0.0 copy-start
  0.6 0.0 copy-start.8
  0.7 0.0 copy-start.4
  0.7 0.0 copy-start.3
  0.7 0.0 copy-start.5
  0.7 0.0 copy-start.6
  0.7 0.0 copy-start.2
  0.7 4.4 %fusion.5 = f32[16,1,96]{2,1,0:T(1,128)S(1)} fusion(f32[16,96,384]{2,1,0:T(8,128)} %param.10, f32[16,384,1]{1,0,2:T(8,128)} %bitcast.43), kind=kOutput, calls=%fused_computation.11 | convolution fusion | flops 7077888 | bytes 2390016 | tf_op jit(solution)/shard_map/zkv,zv->zk/dot_general | solution.py:46
  5.1 0.0 copy-done.8
  5.1 0.3 fusion.8
  5.4 18.1 %psum.14 = f32[4,48]{1,0:T(4,128)S(1)} all-reduce(f32[4,48]{1,0:T(4,128)S(1)} %fusion.8), channel_id=1, replica_groups=mesh['floor'=4,'zone'=8] {'zone'}, use_global_device_ids=true, to_apply=%region_0.0 | all-reduce | flops 192 | bytes 1536 | tf_op jit(solution)/shard_map/psum | solution.py:50
  23.5 0.0 copy-start.1
  23.5 1.5 %collective-permute-start = (f32[4,48]{1,0:T(4,128)S(1)}, f32[4,48]{1,0:T(4,128)S(1)}, u32[]{:S(2)}, u32[]{:S(2)}) collective-permute-start(f32[4,48]{1,0:T(4,128)S(1)} %psum.14), channel_id=1, source_target_pairs={{0,8},{8,0},{16,24},{24,16},{1,9},{9,1},{17,25},{25,17},{2,10},{10... | collective-permute-start | bytes 2312 | tf_op jit(solution)/shard_map/ppermute | solution.py:16
  25.0 0.1 slice.17
  25.1 0.0 copy-done.4
  25.1 0.1 convert_reduce_fusion
  25.2 14.0 %all_gather.6 = f32[128,48]{1,0:T(8,128)S(1)} all-gather(f32[16,48]{1,0:T(8,128)S(1)} %slice.17), channel_id=1, replica_groups=mesh['floor'=4,'zone'=8] {'zone'}, dimensions={0}, use_global_device_ids=true | all-gather | bytes 27648 | tf_op jit(solution)/shard_map/all_gather | solution.py:56
  39.2 0.0 collective-permute-done
  39.2 1.5 %collective-permute-start.1 = (f32[4,48]{1,0:T(4,128)S(1)}, f32[4,48]{1,0:T(4,128)S(1)}, u32[]{:S(2)}, u32[]{:S(2)}) collective-permute-start(f32[4,48]{1,0:T(4,128)S(1)} %add.36), channel_id=1, source_target_pairs={{0,16},{8,24},{16,0},{24,8},{1,17},{9,25},{17,1},{25,9},{2,18},{10... | collective-permute-start | bytes 2312 | tf_op jit(solution)/shard_map/ppermute | solution.py:16
  40.7 0.0 copy-done.3
  40.7 0.2 multiply_subtract_fusion.1
  40.8 1.9 %collective-permute-done.1 = f32[4,48]{1,0:T(4,128)S(1)} collective-permute-done((f32[4,48]{1,0:T(4,128)S(1)}, f32[4,48]{1,0:T(4,128)S(1)}, u32[]{:S(2)}, u32[]{:S(2)}) %collective-permute-start.1) | collective-permute-done | bytes 800 | tf_op jit(solution)/shard_map/ppermute | solution.py:16
  42.7 0.0 copy-done.5
  42.7 0.0 copy-done.6
  42.8 0.2 convolution_subtract_fusion.1
  42.9 0.1 pad_maximum_fusion
  43.0 0.0 copy-done
  43.0 1.4 %fusion.23 = f32[16,1,384]{2,1,0:T(1,128)S(1)} fusion(f32[16,96,1]{1,2,0:T(1,128)S(1)} %bitcast.41, f32[16,96,384]{2,1,0:T(8,128)S(1)} %copy-done), kind=kOutput, calls=%fused_computation.38 | convolution fusion | flops 7077888 | bytes 2390016 | tf_op jit(solution)/shard_map/zkv,zk->zv/dot_general | solution.py:63
  44.5 0.0 copy-done.2
  44.5 0.0 copy-done.1
  44.5 2.6 %fusion.3 = f32[16,1,96]{2,1,0:T(1,128)S(1)} fusion(f32[16,96,384]{2,1,0:T(8,128)S(1)} %copy-done.1, f32[16,384,1]{1,0,2:T(8,128)S(1)} %fusion.2), kind=kOutput, calls=%fused_computation.9 | convolution fusion | flops 7077888 | bytes 2390016 | tf_op jit(solution)/shard_map/zkv,zv->zk/dot_general | solution.py:46
  47.1 0.1 slice.19
  47.2 0.3 fusion.7
  47.4 13.6 %psum.15 = f32[4,48]{1,0:T(4,128)S(1)} all-reduce(f32[4,48]{1,0:T(4,128)S(1)} %fusion.7), channel_id=1, replica_groups=mesh['floor'=4,'zone'=8] {'zone'}, use_global_device_ids=true, to_apply=%region_2.0 | all-reduce | flops 192 | bytes 1536 | tf_op jit(solution)/shard_map/psum | solution.py:50
  61.0 0.6 collective-permute-start.2
  61.6 14.0 %all_gather.7 = f32[128,48]{1,0:T(8,128)S(1)} all-gather(f32[16,48]{1,0:T(8,128)S(1)} %slice.19), channel_id=1, replica_groups=mesh['floor'=4,'zone'=8] {'zone'}, dimensions={0}, use_global_device_ids=true | all-gather | bytes 27648 | tf_op jit(solution)/shard_map/all_gather | solution.py:56
  75.6 0.0 collective-permute-done.2
  75.6 1.5 %collective-permute-start.3 = (f32[4,48]{1,0:T(4,128)S(1)}, f32[4,48]{1,0:T(4,128)S(1)}, u32[]{:S(2)}, u32[]{:S(2)}) collective-permute-start(f32[4,48]{1,0:T(4,128)S(1)} %add.40), channel_id=1, source_target_pairs={{0,16},{8,24},{16,0},{24,8},{1,17},{9,25},{17,1},{25,9},{2,18},{10... | collective-permute-start | bytes 2312 | tf_op jit(solution)/shard_map/ppermute | solution.py:16
  77.1 0.8 multiply_add_fusion
  77.9 1.3 %collective-permute-done.3 = f32[4,48]{1,0:T(4,128)S(1)} collective-permute-done((f32[4,48]{1,0:T(4,128)S(1)}, f32[4,48]{1,0:T(4,128)S(1)}, u32[]{:S(2)}, u32[]{:S(2)}) %collective-permute-start.3) | collective-permute-done | bytes 800 | tf_op jit(solution)/shard_map/ppermute | solution.py:16
  79.2 0.0 copy-start.7
  79.2 0.2 convolution_subtract_fusion
  79.4 0.1 pad_maximum_fusion.1
  79.5 1.4 %fusion.24 = f32[16,1,384]{2,1,0:T(1,128)S(1)} fusion(f32[16,96,1]{1,2,0:T(1,128)S(1)} %bitcast.42, f32[16,96,384]{2,1,0:T(8,128)S(1)} %copy-done), kind=kOutput, calls=%fused_computation.39 | convolution fusion | flops 7077888 | bytes 2390016 | tf_op jit(solution)/shard_map/zkv,zk->zv/dot_general | solution.py:63
  80.9 0.6 fusion
  81.5 0.0 copy-done.7
  (4 shorter events, 0.0 us)
Async XLA Ops:
  0.6 42.4 %copy-start = (f32[16,96,384]{2,1,0:T(8,128)S(1)}, f32[16,96,384]{2,1,0:T(8,128)}, u32[]{:S(2)}) copy-start(f32[16,96,384]{2,1,0:T(8,128)} %param.9) | copy-start | bytes 7077892
  0.6 4.5 %copy-start.8 = (s32[16]{0:T(128)S(1)}, s32[16]{0:T(128)}, u32[]{:S(2)}) copy-start(s32[16]{0:T(128)} %param.17) | copy-start | bytes 196
  0.7 24.4 %copy-start.4 = (s32[16,4]{0,1:T(4,128)S(1)}, s32[16,4]{0,1:T(4,128)}, u32[]{:S(2)}) copy-start(s32[16,4]{0,1:T(4,128)} %param.16) | copy-start | bytes 772
  0.7 40.0 %copy-start.3 = (f32[16,48]{1,0:T(8,128)S(1)}, f32[16,48]{1,0:T(8,128)}, u32[]{:S(2)}) copy-start(f32[16,48]{1,0:T(8,128)} %param.15) | copy-start | bytes 9220
  0.7 42.1 %copy-start.5 = (f32[4,48]{1,0:T(4,128)S(1)}, f32[4,48]{1,0:T(4,128)}, u32[]{:S(2)}) copy-start(f32[4,48]{1,0:T(4,128)} %param.14) | copy-start | bytes 2308
  0.7 42.1 %copy-start.6 = (f32[4,48]{1,0:T(4,128)S(1)}, f32[4,48]{1,0:T(4,128)}, u32[]{:S(2)}) copy-start(f32[4,48]{1,0:T(4,128)} %param.13) | copy-start | bytes 2308
  0.7 43.8 %copy-start.2 = (f32[16,384]{1,0:T(8,128)S(1)}, f32[16,384]{1,0:T(8,128)}, u32[]{:S(2)}) copy-start(f32[16,384]{1,0:T(8,128)} %param.11) | copy-start | bytes 73732
  23.5 21.0 %copy-start.1 = (f32[16,96,384]{2,1,0:T(8,128)S(1)}, f32[16,96,384]{2,1,0:T(8,128)}, u32[]{:S(2)}) copy-start(f32[16,96,384]{2,1,0:T(8,128)} %param.10) | copy-start | bytes 7077892
  23.5 15.7 %collective-permute-start = (f32[4,48]{1,0:T(4,128)S(1)}, f32[4,48]{1,0:T(4,128)S(1)}, u32[]{:S(2)}, u32[]{:S(2)}) collective-permute-start(f32[4,48]{1,0:T(4,128)S(1)} %psum.14), channel_id=1, source_target_pairs={{0,8},{8,0},{16,24},{24,16},{1,9},{9,1},{17,25},{25,17},{2,10},{10... | collective-permute-start | bytes 2312 | tf_op jit(solution)/shard_map/ppermute | solution.py:16
  39.2 3.6 %collective-permute-start.1 = (f32[4,48]{1,0:T(4,128)S(1)}, f32[4,48]{1,0:T(4,128)S(1)}, u32[]{:S(2)}, u32[]{:S(2)}) collective-permute-start(f32[4,48]{1,0:T(4,128)S(1)} %add.36), channel_id=1, source_target_pairs={{0,16},{8,24},{16,0},{24,8},{1,17},{9,25},{17,1},{25,9},{2,18},{10... | collective-permute-start | bytes 2312 | tf_op jit(solution)/shard_map/ppermute | solution.py:16
  61.0 14.6 %collective-permute-start.2 = (f32[4,48]{1,0:T(4,128)S(1)}, f32[4,48]{1,0:T(4,128)S(1)}, u32[]{:S(2)}, u32[]{:S(2)}) collective-permute-start(f32[4,48]{1,0:T(4,128)S(1)} %psum.15), channel_id=1, source_target_pairs={{0,8},{8,0},{16,24},{24,16},{1,9},{9,1},{17,25},{25,17},{2,10},{10... | collective-permute-start | bytes 2312 | tf_op jit(solution)/shard_map/ppermute | solution.py:16
  75.6 3.6 %collective-permute-start.3 = (f32[4,48]{1,0:T(4,128)S(1)}, f32[4,48]{1,0:T(4,128)S(1)}, u32[]{:S(2)}, u32[]{:S(2)}) collective-permute-start(f32[4,48]{1,0:T(4,128)S(1)} %add.40), channel_id=1, source_target_pairs={{0,16},{8,24},{16,0},{24,8},{1,17},{9,25},{17,1},{25,9},{2,18},{10... | collective-permute-start | bytes 2312 | tf_op jit(solution)/shard_map/ppermute | solution.py:16
  79.2 2.3 %copy-start.7 = (f32[4,48]{1,0:T(4,128)}, f32[4,48]{1,0:T(4,128)S(1)}, u32[]{:S(2)}) copy-start(f32[4,48]{1,0:T(4,128)S(1)} %multiply_add_fusion.2) | copy-start | bytes 2308
